TPU v7x, 32 devices: a whole 2x2x4 slice. The times are simulated.
32 devices in a mesh: dp: 8 (over z, core), fsdp: 4 (over y, x).
Axes of the slice: x: 2, y: 2, z: 4, core: 2. Of those that a mesh axis runs over, the one named last changes fastest.
Arguments:
- layer_input_tokens: bfloat16 [32768, 768], P(('dp', 'fsdp')), may hold values from -6 to 6
- cotangent: bfloat16 [32768, 768], P(('dp', 'fsdp')), may hold values from -6 to 6
- lengths: int32 [160], P(('dp', 'fsdp')), may hold values from 33 to 512, as said below
- query_key_value_weight: float32 [768, 2304], P(('dp', 'fsdp')), may hold values from -0.21875 to 0.21875
- output_weight: float32 [768, 768], P(('dp', 'fsdp')), may hold values from -0.875 to 0.875
- up_weight: float32 [768, 3072], P(('dp', 'fsdp')), may hold values from -0.21875 to 0.21875
- down_weight: float32 [3072, 768], P(('dp', 'fsdp')), may hold values from -0.109375 to 0.109375
- a_in: float32 [768, 40], P(('dp', 'fsdp')), may hold values from -0.21875 to 0.21875
- a_down: float32 [3072, 8], P(('dp', 'fsdp')), may hold values from -0.109375 to 0.109375
- ln_gains: float32 [2, 768], P(None, ('dp', 'fsdp')), may hold values from 0.5 to 1.5
- ln_biases: float32 [2, 768], P(None, ('dp', 'fsdp')), may hold values from -3 to 3
- adapter_b: float32 [8, 6912], replicated, may hold values from -0.3 to 0.3
- moment_one: float32 [8, 6912], replicated, may hold values from -0.72 to 0.72
- moment_two: float32 [8, 6912], replicated, may hold values from 0.005 to 0.05
Outputs:
- layer_out: bfloat16 [32768, 768], P(('dp', 'fsdp'))
- input_grad: bfloat16 [32768, 768], P(('dp', 'fsdp'))
- b_grad: float32 [8, 6912], replicated
- grad_norm: float32 [], replicated
- moment_one_new: float32 [8, 6912], replicated
- moment_two_new: float32 [8, 6912], replicated
- adapter_b_new: float32 [8, 6912], replicated
Inputs may be any that keep to these rules, and one draw needn't show every extreme that they name: `lengths`: item 5 j + i lies in bucket i of its set; its length is more than half of its bucket and at most the bucket. Some item has exactly 512 valid tokens.
All inputs are finite; a program needn't handle non-finite values.
Results may differ from a plain program's by a relative error of at most 0.012.
The roundings to bfloat16 on the way count: a program that leaves them out, or rounds other values in their place, can miss the bound.
Values may be sent and summed in bfloat16 or wider, within the bound.
A program may use at most 192 MiB of HBM per device.

v0:
```python
import jax
import jax.numpy as jnp
from jax import lax
from jax.sharding import PartitionSpec as P

HEAD = 64
ITEM_LEN = 512
STEP = 10
adapter_scale = 2.0
ln_eps = 1e-05
clip_norm = 256.0
beta_one = 0.9
beta_two = 0.98
learn_rate = 0.02
decay_rate = 0.01


def bucket_plan(full):
    return (
        (0, full, 1, 0),
        (full, full // 2, 1, 1),
        (full * 3 // 2, full // 4, 1, 2),
        (full * 7 // 4, full // 8, 2, 3),
    )


def keep_mask(lengths_set, full):
    parts = []
    for offset, size, count, first in bucket_plan(full):
        positions = jnp.arange(size, dtype=jnp.int32)
        bounds = lengths_set[:, first : first + count]
        mask = (positions[None, None, :] < bounds[:, :, None]).astype(jnp.float32)
        parts.append(mask.reshape(lengths_set.shape[0], count * size))
    return jnp.concatenate(parts, axis=1)


def product_result(left, right):
    return jnp.dot(left, right, preferred_element_type=jnp.float32)


def transposed_product(left, right):
    return lax.dot_general(
        left, right, (((1,), (1,)), ((), ())), preferred_element_type=jnp.float32
    )


def product_tn(left, right):
    return lax.dot_general(
        left, right, (((0,), (0,)), ((), ())), preferred_element_type=jnp.float32
    )


def norm_forward(resid, gain, shift):
    center = resid - jnp.mean(resid, axis=1, keepdims=True)
    variance = jnp.mean(center * center, axis=1, keepdims=True)
    inv_std = lax.rsqrt(variance + ln_eps)
    normed = center * inv_std
    return (normed * gain + shift, normed, inv_std)


def norm_backward(grad_out, normed, inv_std, gain):
    scaled = grad_out * gain
    return inv_std * (
        scaled
        - jnp.mean(scaled, axis=1, keepdims=True)
        - normed * jnp.mean(scaled * normed, axis=1, keepdims=True)
    )


def gelu_exact(values):
    return 0.5 * values * (1.0 + jax.scipy.special.erf(values * 0.7071067811865476))


def gelu_slope(values):
    normal_cdf = 0.5 * (1.0 + jax.scipy.special.erf(values * 0.7071067811865476))
    density = jnp.exp(-0.5 * values * values) * 0.3989422804014327
    return normal_cdf + values * density


def masked_scores(query, key_rows, keep_block):
    scores = (
        jnp.einsum("gqhe,gkhe->ghqk", query, key_rows, preferred_element_type=jnp.float32) * 0.125
    )
    return jnp.where(keep_block[:, None, None, :] > 0.5, scores, -1e30)


def bucket_forward(query, key_rows, value_rows, keep_block):
    scores = masked_scores(query, key_rows, keep_block)
    highest = jnp.max(scores, axis=-1, keepdims=True)
    expo = jnp.exp(scores - highest)
    totals = jnp.sum(expo, axis=-1, keepdims=True)
    probs = (expo / totals).astype(jnp.bfloat16)
    context_rows = jnp.einsum(
        "ghqk,gkhe->gqhe", probs, value_rows, preferred_element_type=jnp.float32
    )
    return (context_rows.astype(jnp.bfloat16), highest + jnp.log(totals))


def bucket_backward(query, key_rows, value_rows, keep_block, log_total, grad_ctx):
    scores = masked_scores(query, key_rows, keep_block)
    probs = jnp.exp(scores - log_total)
    grad_probs = jnp.einsum(
        "gqhe,gkhe->ghqk", grad_ctx, value_rows, preferred_element_type=jnp.float32
    )
    delta = jnp.sum(probs * grad_probs, axis=-1, keepdims=True)
    grad_scores = (probs * (grad_probs - delta)).astype(jnp.bfloat16)
    grad_query = (
        jnp.einsum("ghqk,gkhe->gqhe", grad_scores, key_rows, preferred_element_type=jnp.float32)
        * 0.125
    )
    grad_key = (
        jnp.einsum("ghqk,gqhe->gkhe", grad_scores, query, preferred_element_type=jnp.float32)
        * 0.125
    )
    grad_value = jnp.einsum(
        "ghqk,gqhe->gkhe", probs.astype(jnp.bfloat16), grad_ctx, preferred_element_type=jnp.float32
    )
    return (
        grad_query.astype(jnp.bfloat16),
        grad_key.astype(jnp.bfloat16),
        grad_value.astype(jnp.bfloat16),
    )


def set_forward(operands):
    query, key_rows, value_rows, lens = operands
    heads, size_head = (query.shape[1], query.shape[2])
    keep_set = keep_mask(lens[None, :], ITEM_LEN)[0]
    contexts = []
    totals = []
    for offset, size, count, first in bucket_plan(ITEM_LEN):
        span = count * size
        shape = (count, size, heads, size_head)
        context_rows, log_total = bucket_forward(
            query[offset : offset + span].reshape(shape),
            key_rows[offset : offset + span].reshape(shape),
            value_rows[offset : offset + span].reshape(shape),
            keep_set[offset : offset + span].reshape(count, size),
        )
        contexts.append(context_rows.reshape(span, heads, size_head))
        totals.append(log_total)
    return (jnp.concatenate(contexts, axis=0), tuple(totals))


def set_backward(operands):
    query, key_rows, value_rows, lens, log_totals, grad_ctx = operands
    heads, size_head = (query.shape[1], query.shape[2])
    keep_set = keep_mask(lens[None, :], ITEM_LEN)[0]
    grads_q = []
    grads_k = []
    grads_v = []
    for index, (offset, size, count, first) in enumerate(bucket_plan(ITEM_LEN)):
        span = count * size
        shape = (count, size, heads, size_head)
        grad_q, grad_k, grad_v = bucket_backward(
            query[offset : offset + span].reshape(shape),
            key_rows[offset : offset + span].reshape(shape),
            value_rows[offset : offset + span].reshape(shape),
            keep_set[offset : offset + span].reshape(count, size),
            log_totals[index],
            grad_ctx[offset : offset + span].reshape(shape),
        )
        grads_q.append(grad_q.reshape(span, heads, size_head))
        grads_k.append(grad_k.reshape(span, heads, size_head))
        grads_v.append(grad_v.reshape(span, heads, size_head))
    return (
        jnp.concatenate(grads_q, axis=0),
        jnp.concatenate(grads_k, axis=0),
        jnp.concatenate(grads_v, axis=0),
    )


def adam_update(gradient, grad_norm, moment_old, second_old, weights):
    clipped = gradient * jnp.minimum(1.0, clip_norm / (grad_norm + 1e-06))
    moment_new = beta_one * moment_old + (1.0 - beta_one) * clipped
    second_new = beta_two * second_old + (1.0 - beta_two) * clipped * clipped
    first_hat = moment_new / (1.0 - beta_one**STEP)
    second_hat = second_new / (1.0 - beta_two**STEP)
    weights_new = weights - learn_rate * (
        first_hat / (jnp.sqrt(second_hat) + 1e-08) + decay_rate * weights
    )
    return (moment_new, second_new, weights_new)


def on_device(
    layer_input_tokens,
    cotangent,
    lengths,
    query_key_value_weight,
    output_weight,
    up_weight,
    down_weight,
    a_in,
    a_down,
    ln_gains,
    ln_biases,
    adapter_b,
    moment_one,
    moment_two,
):
    total_rows, width = layer_input_tokens.shape
    span_all = 2 * ITEM_LEN
    sets = total_rows // span_all
    lowrank = adapter_b.shape[0]
    hidden = up_weight.shape[1]
    head_count = width // HEAD
    brain_float_type = jnp.bfloat16
    gathered = (
        lax.all_gather(
            query_key_value_weight.astype(brain_float_type), ("dp", "fsdp"), axis=0, tiled=True
        ),
        lax.all_gather(output_weight.astype(brain_float_type), ("dp", "fsdp"), axis=0, tiled=True),
        lax.all_gather(up_weight.astype(brain_float_type), ("dp", "fsdp"), axis=0, tiled=True),
        lax.all_gather(down_weight.astype(brain_float_type), ("dp", "fsdp"), axis=0, tiled=True),
        lax.all_gather(a_in.astype(brain_float_type), ("dp", "fsdp"), axis=0, tiled=True),
        lax.all_gather(a_down.astype(brain_float_type), ("dp", "fsdp"), axis=0, tiled=True),
        lax.all_gather(ln_gains.astype(brain_float_type), ("dp", "fsdp"), axis=1, tiled=True),
        lax.all_gather(ln_biases.astype(brain_float_type), ("dp", "fsdp"), axis=1, tiled=True),
    )
    (
        projection_weight_gradient,
        output_weight_gradient,
        up_weight_gradient,
        down_weight_gradient,
        g_ain,
        g_adown,
        g_gain,
        g_bias,
    ) = gathered
    gain_full = g_gain.astype(jnp.float32)
    bias_full = g_bias.astype(jnp.float32)
    lengths_set = lengths.reshape(sets, 5)
    keep = keep_mask(lengths_set, ITEM_LEN)
    keep_rows = keep.reshape(-1, 1)
    b_low = adapter_b.astype(brain_float_type)
    query_adapter_matrix = b_low[:, :width]
    key_adapter_matrix = b_low[:, width : 2 * width]
    value_adapter_matrix = b_low[:, 2 * width : 3 * width]
    attention_adapter_bias = b_low[:, 3 * width : 4 * width]
    upper_adapter_matrix = b_low[:, 4 * width : 4 * width + hidden]
    lower_adapter_matrix = b_low[:, 4 * width + hidden :]
    projection_down_matrix = product_result(layer_input_tokens, g_ain[:, : 3 * lowrank]).astype(
        brain_float_type
    )
    adapter_projection_delta = jnp.concatenate(
        [
            product_result(projection_down_matrix[:, :lowrank], query_adapter_matrix),
            product_result(projection_down_matrix[:, lowrank : 2 * lowrank], key_adapter_matrix),
            product_result(projection_down_matrix[:, 2 * lowrank :], value_adapter_matrix),
        ],
        axis=1,
    )
    query_key_value = (
        product_result(layer_input_tokens, projection_weight_gradient)
        + adapter_scale * adapter_projection_delta
    ).astype(brain_float_type)
    qkv_heads = query_key_value.reshape(sets, span_all, 3, head_count, HEAD)
    query = qkv_heads[:, :, 0]
    key_rows = qkv_heads[:, :, 1]
    value_rows = qkv_heads[:, :, 2]
    context_rows, log_totals = lax.map(set_forward, (query, key_rows, value_rows, lengths_set))
    context_token_rows = context_rows.reshape(sets * span_all, width)
    attention_down_matrix = product_result(
        context_token_rows, g_ain[:, 3 * lowrank : 4 * lowrank]
    ).astype(brain_float_type)
    attention_output = product_result(
        context_token_rows, output_weight_gradient
    ) + adapter_scale * product_result(attention_down_matrix, attention_adapter_bias)
    hidden_one, normed_one, inv_one = norm_forward(
        layer_input_tokens.astype(jnp.float32) + attention_output, gain_full[0], bias_full[0]
    )
    hidden_lower_rows = hidden_one.astype(brain_float_type)
    upper_down_matrix = product_result(hidden_lower_rows, g_ain[:, 4 * lowrank :]).astype(
        brain_float_type
    )
    upper_rows = product_result(
        hidden_lower_rows, up_weight_gradient
    ) + adapter_scale * product_result(upper_down_matrix, upper_adapter_matrix)
    active_rows = gelu_exact(upper_rows).astype(brain_float_type)
    lower_down_matrix = product_result(active_rows, g_adown).astype(brain_float_type)
    feedforward_output = product_result(
        active_rows, down_weight_gradient
    ) + adapter_scale * product_result(lower_down_matrix, lower_adapter_matrix)
    output, normed_two, inv_two = norm_forward(
        hidden_one + feedforward_output, gain_full[1], bias_full[1]
    )
    layer_out = (output * keep_rows).astype(brain_float_type)
    again = (
        lax.all_gather(
            query_key_value_weight.astype(brain_float_type), ("dp", "fsdp"), axis=0, tiled=True
        ),
        lax.all_gather(output_weight.astype(brain_float_type), ("dp", "fsdp"), axis=0, tiled=True),
        lax.all_gather(up_weight.astype(brain_float_type), ("dp", "fsdp"), axis=0, tiled=True),
        lax.all_gather(down_weight.astype(brain_float_type), ("dp", "fsdp"), axis=0, tiled=True),
        lax.all_gather(a_in.astype(brain_float_type), ("dp", "fsdp"), axis=0, tiled=True),
        lax.all_gather(a_down.astype(brain_float_type), ("dp", "fsdp"), axis=0, tiled=True),
        lax.all_gather(ln_gains.astype(brain_float_type), ("dp", "fsdp"), axis=1, tiled=True),
        lax.all_gather(ln_biases.astype(brain_float_type), ("dp", "fsdp"), axis=1, tiled=True),
    )
    (
        projection_weight_gradient,
        output_weight_gradient,
        up_weight_gradient,
        down_weight_gradient,
        g_ain,
        g_adown,
        g_gain,
        g_bias,
    ) = again
    gain_full = g_gain.astype(jnp.float32)
    grad_out = cotangent.astype(jnp.float32) * keep_rows
    grad_two = norm_backward(grad_out, normed_two, inv_two, gain_full[1])
    feedforward_gradient = grad_two.astype(brain_float_type)
    lower_down_gradient = (
        adapter_scale * transposed_product(feedforward_gradient, lower_adapter_matrix)
    ).astype(brain_float_type)
    grad_active = transposed_product(
        feedforward_gradient, down_weight_gradient
    ) + transposed_product(lower_down_gradient, g_adown)
    upper_output_gradient = (grad_active * gelu_slope(upper_rows)).astype(brain_float_type)
    upper_down_gradient = (
        adapter_scale * transposed_product(upper_output_gradient, upper_adapter_matrix)
    ).astype(brain_float_type)
    grad_hidden = (
        grad_two
        + transposed_product(upper_output_gradient, up_weight_gradient)
        + transposed_product(upper_down_gradient, g_ain[:, 4 * lowrank :])
    )
    grad_one = norm_backward(grad_hidden, normed_one, inv_one, gain_full[0])
    attention_gradient = grad_one.astype(brain_float_type)
    attention_down_gradient = (
        adapter_scale * transposed_product(attention_gradient, attention_adapter_bias)
    ).astype(brain_float_type)
    grad_ctx = (
        transposed_product(attention_gradient, output_weight_gradient)
        + transposed_product(attention_down_gradient, g_ain[:, 3 * lowrank : 4 * lowrank])
    ).astype(brain_float_type)
    grad_q, grad_k, grad_v = lax.map(
        set_backward,
        (
            query,
            key_rows,
            value_rows,
            lengths_set,
            log_totals,
            grad_ctx.reshape(sets, span_all, head_count, HEAD),
        ),
    )
    grad_qkv = jnp.stack([grad_q, grad_k, grad_v], axis=2).reshape(sets * span_all, 3 * width)
    grad_uqkv = (
        adapter_scale
        * jnp.concatenate(
            [
                transposed_product(grad_qkv[:, :width], query_adapter_matrix),
                transposed_product(grad_qkv[:, width : 2 * width], key_adapter_matrix),
                transposed_product(grad_qkv[:, 2 * width :], value_adapter_matrix),
            ],
            axis=1,
        )
    ).astype(brain_float_type)
    input_grad = (
        grad_one
        + transposed_product(grad_qkv, projection_weight_gradient)
        + transposed_product(grad_uqkv, g_ain[:, : 3 * lowrank])
    ).astype(brain_float_type)
    local_gradient = adapter_scale * jnp.concatenate(
        [
            product_tn(projection_down_matrix[:, :lowrank], grad_qkv[:, :width]),
            product_tn(
                projection_down_matrix[:, lowrank : 2 * lowrank], grad_qkv[:, width : 2 * width]
            ),
            product_tn(projection_down_matrix[:, 2 * lowrank :], grad_qkv[:, 2 * width :]),
            product_tn(attention_down_matrix, attention_gradient),
            product_tn(upper_down_matrix, upper_output_gradient),
            product_tn(lower_down_matrix, feedforward_gradient),
        ],
        axis=1,
    )
    b_grad = lax.psum(local_gradient, ("dp", "fsdp"))
    grad_norm = jnp.sqrt(jnp.sum(b_grad * b_grad))
    moment_new, second_new, adapter_new = adam_update(
        b_grad, grad_norm, moment_one, moment_two, adapter_b
    )
    return (layer_out, input_grad, b_grad, grad_norm, moment_new, second_new, adapter_new)


def solution(mesh):
    placed = (
        P(("dp", "fsdp"), None),
        P(("dp", "fsdp"), None),
        P(("dp", "fsdp")),
        P(("dp", "fsdp"), None),
        P(("dp", "fsdp"), None),
        P(("dp", "fsdp"), None),
        P(("dp", "fsdp"), None),
        P(("dp", "fsdp"), None),
        P(("dp", "fsdp"), None),
        P(None, ("dp", "fsdp")),
        P(None, ("dp", "fsdp")),
        P(),
        P(),
        P(),
    )
    return jax.shard_map(
        on_device,
        mesh=mesh,
        in_specs=placed,
        out_specs=(P(("dp", "fsdp"), None), P(("dp", "fsdp"), None), P(), P(), P(), P(), P()),
        check_vma=False,
    )
```

profile of v0, /device:TPU:8, one launch (start us, length us, event | category | flops | bytes accessed | tf_op | source)
XLA Modules:
  0.0 654.7 jit_solution(7428954899423333268)
XLA Ops:
  22.8 57.2 %all_gather.32 = bf16[768,40]{1,0:T(8,128)(2,1)S(1)} all-gather(bf16[24,40]{1,0:T(8,128)(2,1)S(1)} %convert_element_type.393), channel_id=1, replica_groups=mesh['dp'=8,'fsdp'=4] {'dp','fsdp'}, dimensions={0}, use_global_device_ids=true | all-gather | bytes 63360 | tf_op jit(solution)/shard_map/all_gather | solution.py:215
  89.9 64.0 %all-gather.1 = bf16[32,24,2]{1,2,0:T(2,128)(2,1)S(1)} all-gather(bf16[1,24,2]{1,2,0:T(2,128)(2,1)S(1)} %convert_bitcast_fusion.1), channel_id=1, replica_groups=mesh['dp'=8,'fsdp'=4] {'dp','fsdp'}, dimensions={0}, use_global_device_ids=true | all-gather | bytes 3168 | tf_op jit(solution)/shard_map/all_gather | solution.py:218
  154.0 66.0 %all-gather = bf16[32,24,2]{1,2,0:T(2,128)(2,1)S(1)} all-gather(bf16[1,24,2]{1,2,0:T(2,128)(2,1)S(1)} %convert_bitcast_fusion.2), channel_id=1, replica_groups=mesh['dp'=8,'fsdp'=4] {'dp','fsdp'}, dimensions={0}, use_global_device_ids=true | all-gather | bytes 3168 | tf_op jit(solution)/shard_map/all_gather | solution.py:217
  221.7 63.5 %all-gather.2 = bf16[32,96,8]{1,2,0:T(8,128)(2,1)S(1)} all-gather(bf16[1,96,8]{1,2,0:T(8,128)(2,1)S(1)} %convert_bitcast_fusion), channel_id=1, replica_groups=mesh['dp'=8,'fsdp'=4] {'dp','fsdp'}, dimensions={0}, use_global_device_ids=true | all-gather | bytes 50688 | tf_op jit(solution)/shard_map/all_gather | solution.py:216
  288.1 8.8 %fusion.9 = bf16[1024,2304]{1,0:T(8,128)(2,1)} fusion(f32[1024,768]{1,0:T(8,128)} %fusion.119, f32[1024,768]{1,0:T(8,128)} %fusion.122, f32[1024,768]{1,0:T(8,128)} %fusion.125, bf16[1024,768]{1,0:T(8,128)(2,1)S(1)} %copy-done.17, bf16[768,2304]{1,0:T(8,128)(2,1)} %all-gather.8.cloned.1.call-done), kind=kOutput, calls=%fused_computation.20 | convolution fusion | flops 3635675136 | bytes 19267584 | tf_op jit(solution)/shard_map/dot_general | solution.py:38
  297.0 6.6 %copy.153 = bf16[1024,2304]{0,1:T(8,128)(2,1)} copy(bf16[1024,2304]{1,0:T(8,128)(2,1)} %fusion.9) | data formatting | bytes 9437184 | tf_op jit(solution)/shard_map/convert_element_type | solution.py:256
  314.2 5.1 fusion.157
  325.5 4.0 fusion.25
  338.4 7.5 %fusion.162 = f32[1024,3072]{1,0:T(8,128)S(1)} fusion(bf16[1024,768]{0,1:T(8,128)(2,1)} %copy-done.8, bf16[768,3072]{1,0:T(8,128)(2,1)} %all-gather.12.cloned.1.call-done), kind=kOutput, calls=%fused_computation.253 | convolution fusion | flops 4831838208 | bytes 18874368 | tf_op jit(solution)/shard_map/dot_general | solution.py:38
  345.9 7.2 %multiply_convert_fusion.1 = (bf16[1024,3072]{1,0:T(8,128)(2,1)S(1)}, f32[1024,3072]{1,0:T(8,128)}) fusion(f32[1024,3072]{1,0:T(8,128)S(1)} %fusion.162, bf16[1024,8]{0,1:T(8,128)(2,1)S(1)} %convolution_convert_fusion.6, bf16[8,6912]{1,0:T(8,128)(2,1)S(1)} %convert_element_type.395), kind=kOutput, calls=%fused_computation.10 | convolution fusion | flops 72351744 | bytes 31522816 | tf_op jit(solution)/shard_map/dot_general | solution.py:38
  357.5 8.8 %fusion.163 = f32[1024,768]{0,1:T(8,128)S(1)} fusion(bf16[1024,3072]{1,0:T(8,128)(2,1)} %copy-done.6, bf16[3072,768]{1,0:T(8,128)(2,1)} %all-gather.14.cloned.1.call-done), kind=kOutput, calls=%fused_computation.254 | convolution fusion | flops 4831838208 | bytes 14155776 | tf_op jit(solution)/shard_map/dot_general | solution.py:38
  373.5 8.0 %fusion.164 = f32[1024,3072]{1,0:T(8,128)} fusion(bf16[1024,768]{0,1:T(8,128)(2,1)S(1)} %get-tuple-element.118, bf16[3072,768]{1,0:T(8,128)(2,1)S(1)} %bitcast.280), kind=kOutput, calls=%fused_computation.255 | convolution fusion | flops 4831838208 | bytes 18874368 | tf_op jit(solution)/shard_map/dot_general | solution.py:42
  381.5 13.7 %fusion.5 = bf16[1024,3072]{1,0:T(8,128)(2,1)} fusion(f32[1024,3072]{1,0:T(8,128)} %get-tuple-element.136, f32[1024,3072]{1,0:T(8,128)} %fusion.164, bf16[3072,8]{0,1:T(8,128)(2,1)S(1)} %copy-done.47, bf16[1024,768]{0,1:T(8,128)(2,1)} %copy-done.18, bf16[8,6912]{1,0:T(8,128)(2,1)S(1)} %convert_element_type.395), kind=kOutput, calls=%fused_computation.6 | convolution fusion | flops 97533952 | bytes 33091584 | tf_op jit(solution)/shard_map/dot_general | solution.py:42
  395.2 10.0 %fusion.165 = f32[1024,768]{0,1:T(8,128)} fusion(bf16[1024,3072]{1,0:T(8,128)(2,1)} %fusion.5, bf16[768,3072]{1,0:T(8,128)(2,1)} %all-gather.12.cloned.1.call-done), kind=kOutput, calls=%fused_computation.256 | convolution fusion | flops 4831838208 | bytes 14155776 | tf_op jit(solution)/shard_map/dot_general | solution.py:42
  405.2 10.2 %fusion.149 = (f32[1024]{0:T(1024)S(1)}, f32[1024]{0:T(1024)S(1)}, f32[1024,768]{0,1:T(8,128)}) fusion(f32[1024]{0:T(1024)S(1)} %copy-done.53, f32[1024,768]{0,1:T(8,128)S(1)} %get-tuple-element.134, f32[1024]{0:T(1024)S(1)} %broadcast_multiply_fusion.6, f32[768]{0:T(1024)S(1)} %copy-done.62, bf16[768,40]{1,0:T(8,128)(2,1)S(1)} %all_gather.32, ...), kind=kOutput, calls=%fused_computation.243 | convolution fusion | flops 76298240 | bytes 20738048 | tf_op jit(solution)/shard_map/dot_general | solution.py:42
  419.5 3.0 fusion.166
  422.5 4.4 add_convert_fusion.1
  455.5 3.2 fusion.38
  458.7 7.1 %multiply_reduce_fusion = (f32[12,512]{1,0:T(8,128)S(1)}, f32[12,512,512]{1,2,0:T(8,128)}) fusion(f32[12,512,512]{1,2,0:T(8,128)S(1)} %bitcast.240, f32[12,512]{1,0:T(8,128)S(1)} %copy-done.39, bf16[512,12,64]{0,2,1:T(8,128)(2,1)S(1)} %bitcast.267, bf16[1,1024,3,12,64]{1,4,3,2,0:T(8,128)(2,1)} %bitcast.254), kind=kOutput, calls=%fused_computation.8 | convolution fusion | flops 412084224 | bytes 26787840 | tf_op jit(solution)/shard_map/while/body/eval_jaxpr/gqhe,gkhe->ghqk/dot_general | solution.py:102
  465.8 6.8 %multiply_convert_fusion = bf16[12,512,512]{1,2,0:T(8,128)(2,1)S(1)} fusion(f32[12,512,512]{1,2,0:T(8,128)} %get-tuple-element.147, f32[12,512,512]{1,2,0:T(8,128)S(1)} %bitcast.240, f32[12,512]{1,0:T(8,128)S(1)} %get-tuple-element.146, f32[12,512]{1,0:T(8,128)S(1)} %copy-done.39), kind=kLoop, calls=%fused_computation.7 | loop fusion | flops 12582912 | bytes 31506432 | tf_op jit(solution)/shard_map/while/body/eval_jaxpr/convert_element_type | solution.py:106
  472.6 4.0 fusion.43
  476.7 3.1 fusion.42
  503.4 6.9 %fusion.167 = f32[1024,768]{0,1:T(8,128)S(1)} fusion(bf16[768,2304]{1,0:T(8,128)(2,1)} %all-gather.8.cloned.1.call-done, bf16[1024,2304]{0,1:T(8,128)(2,1)} %bitcast.265), kind=kOutput, calls=%fused_computation.258 | convolution fusion | flops 3623878656 | bytes 11403264 | tf_op jit(solution)/shard_map/dot_general | solution.py:42
  517.0 123.7 %all-reduce.2.cloned.1.call-done = f32[8,6912]{1,0:T(8,128)} async-done(((f32[8,6912]{1,0:T(8,128)}), f32[8,6912]{1,0:T(8,128)}) %all-reduce.2.cloned.1.call-update) | async-done | bytes 221200 | tf_op jit(solution)/shard_map/psum | solution.py:379
  (324 shorter events, 134.5 us)
Async XLA Ops:
  7.2 72.8 %copy-start.17 = (bf16[1024,768]{1,0:T(8,128)(2,1)S(1)}, bf16[1024,768]{1,0:T(8,128)(2,1)}, u32[]{:S(2)}) copy-start(bf16[1024,768]{1,0:T(8,128)(2,1)} %param.14) | copy-start | bytes 4718596
  7.2 281.0 %all-gather.8.cloned.1.call-start = ((), (), s32[]{:S(2)}) async-start(), calls=%async_computation | async-start | bytes 3649536 | tf_op jit(solution)/shard_map/all_gather | solution.py:209
  8.9 321.0 %all-gather.10.cloned.1.call-start = ((), (), s32[]{:S(2)}) async-start(), calls=%async_computation.1 | async-start | bytes 1216512 | tf_op jit(solution)/shard_map/all_gather | solution.py:212
  10.5 327.8 %all-gather.12.cloned.1.call-start = ((), (), s32[]{:S(2)}) async-start(), calls=%async_computation.2 | async-start | bytes 4866048 | tf_op jit(solution)/shard_map/all_gather | solution.py:213
  12.2 345.3 %all-gather.14.cloned.1.call-start = ((), (), s32[]{:S(2)}) async-start(), calls=%async_computation.3 | async-start | bytes 4866048 | tf_op jit(solution)/shard_map/all_gather | solution.py:214
  13.9 626.8 %all-reduce.2.cloned.1.call-start = ((), (), s32[]{:S(2)}) async-start(), calls=%async_computation.4 | async-start | bytes 442368 | tf_op jit(solution)/shard_map/psum | solution.py:379
  22.8 399.7 %copy-start.38 = (bf16[8,6912]{1,0:T(8,128)(2,1)}, bf16[8,6912]{1,0:T(8,128)(2,1)S(1)}, u32[]{:S(2)}) copy-start(bf16[8,6912]{1,0:T(8,128)(2,1)S(1)} %convert_element_type.395) | copy-start | bytes 331780
  84.4 201.5 %copy-start.26 = (bf16[1024,768]{1,0:T(8,128)(2,1)S(1)}, bf16[1024,768]{1,0:T(8,128)(2,1)}, u32[]{:S(2)}) copy-start(bf16[1024,768]{1,0:T(8,128)(2,1)} %param.15) | copy-start | bytes 4718596
  220.9 115.4 %copy-start.61 = (f32[768]{0:T(1024)}, f32[768]{0:T(1024)S(1)}, u32[]{:S(2)}) copy-start(f32[768]{0:T(1024)S(1)} %get-tuple-element.109) | copy-start | bytes 9220
  333.8 81.7 %copy-start.45 = (f32[1024]{0:T(1024)}, f32[1024]{0:T(1024)S(1)}, u32[]{:S(2)}) copy-start(f32[1024]{0:T(1024)S(1)} %broadcast_multiply_fusion.6) | copy-start | bytes 12292
  338.3 7.5 %copy-start.48 = (bf16[1024,8]{0,1:T(8,128)(2,1)}, bf16[1024,8]{0,1:T(8,128)(2,1)S(1)}, u32[]{:S(2)}) copy-start(bf16[1024,8]{0,1:T(8,128)(2,1)S(1)} %convolution_convert_fusion.6) | copy-start | bytes 49156
  345.9 9.9 %copy-start.47 = (bf16[3072,8]{0,1:T(8,128)(2,1)S(1)}, bf16[3072,8]{0,1:T(8,128)(2,1)}, u32[]{:S(2)}) copy-start(bf16[3072,8]{0,1:T(8,128)(2,1)} %reshape.756) | copy-start | bytes 147460
  357.5 8.9 %copy-start.50 = (bf16[1024,8]{0,1:T(8,128)(2,1)}, bf16[1024,8]{0,1:T(8,128)(2,1)S(1)}, u32[]{:S(2)}) copy-start(bf16[1024,8]{0,1:T(8,128)(2,1)S(1)} %convolution_convert_fusion.5) | copy-start | bytes 49156
  357.5 8.9 %copy-start.53 = (f32[1024]{0:T(1024)S(1)}, f32[1024]{0:T(1024)}, u32[]{:S(2)}) copy-start(f32[1024]{0:T(1024)} %copy-done.52) | copy-start | bytes 12292
  357.5 8.9 %copy-start.62 = (f32[768]{0:T(1024)S(1)}, f32[768]{0:T(1024)}, u32[]{:S(2)}) copy-start(f32[768]{0:T(1024)} %copy-done.61) | copy-start | bytes 9220
  357.5 8.9 %copy-start.69 = (f32[768]{0:T(1024)S(1)}, f32[768]{0:T(1024)}, u32[]{:S(2)}) copy-start(f32[768]{0:T(1024)} %get-tuple-element.111) | copy-start | bytes 9220
  373.5 8.0 %copy-start.18 = (bf16[1024,768]{0,1:T(8,128)(2,1)}, bf16[1024,768]{0,1:T(8,128)(2,1)S(1)}, u32[]{:S(2)}) copy-start(bf16[1024,768]{0,1:T(8,128)(2,1)S(1)} %get-tuple-element.118) | copy-start | bytes 4718596
  446.7 8.8 %slice-start = ((s8[12582912]{0:T(1024)(128)(4,1)}), s8[4194304]{0:T(1024)(128)(4,1)S(1)}, s32[]{:S(2)}) async-start(s8[12582912]{0:T(1024)(128)(4,1)} %bitcast.239), calls=%async_computation.5 | async-start | bytes 8388608
  448.1 7.4 %slice-start.1 = ((s8[12582912]{0:T(1024)(128)(4,1)}), s8[4194304]{0:T(1024)(128)(4,1)S(1)}, s32[]{:S(2)}) async-start(s8[12582912]{0:T(1024)(128)(4,1)} %bitcast.239), calls=%async_computation.6 | async-start | bytes 8388608
  479.8 10.7 %copy-start.33 = (bf16[128,12,64]{0,2,1:T(8,128)(2,1)S(1)}, bf16[128,12,64]{0,2,1:T(8,128)(2,1)}, u32[]{:S(2)}) copy-start(bf16[128,12,64]{0,2,1:T(8,128)(2,1)} %fusion.66) | copy-start | bytes 589828
  493.0 7.7 %slice-start.3 = ((s8[6291456]{0:T(1024)(128)(4,1)}), s8[2097152]{0:T(1024)(128)(4,1)S(1)}, s32[]{:S(2)}) async-start(s8[6291456]{0:T(1024)(128)(4,1)} %bitcast.257), calls=%async_computation.8 | async-start | bytes 4194304
  512.7 130.3 %copy-start.32 = (f32[8,6912]{1,0:T(8,128)S(1)}, f32[8,6912]{1,0:T(8,128)}, u32[]{:S(2)}) copy-start(f32[8,6912]{1,0:T(8,128)} %param.25) | copy-start | bytes 663556
  512.7 130.3 %copy-start.43 = (f32[8,6912]{1,0:T(8,128)S(1)}, f32[8,6912]{1,0:T(8,128)}, u32[]{:S(2)}) copy-start(f32[8,6912]{1,0:T(8,128)} %param.27) | copy-start | bytes 663556
  512.7 130.4 %copy-start.44 = (f32[8,6912]{1,0:T(8,128)S(1)}, f32[8,6912]{1,0:T(8,128)}, u32[]{:S(2)}) copy-start(f32[8,6912]{1,0:T(8,128)} %param.26) | copy-start | bytes 663556
  (72 other events, 252.4 us)
Sparse Core Ops, SparseCore 0:
  11.4 60.8 all-gather.7
  75.2 52.5 all-gather.9
  131.3 63.4 all-gather.11
  198.1 62.1 all-gather.13
  503.5 137.1 all-reduce.1
where the time goes:
time: 659 us; the launch traced here: 655 us
  blocking collectives  251 us (38%)
  matrix products  168 us (25%)
  waiting for transfers between devices  124 us (19%)
  local copies, waits for them, and re-layouts  54 us (8%)
  other arithmetic  41 us (6%)
  between operations  17.3 us (3%)
    psum x1, waiting for transfers between devices, on_device(): b_grad = lax.psum(local_gradient, ('dp', 'fsdp'))  124 us
    all_gather x1, blocking collectives, on_device(): lax.all_gather(ln_gains.astype(brain_float_type), ('dp', 'fsdp'), axis=1,...  66 us
    all_gather x1, blocking collectives, on_device(): lax.all_gather(ln_biases.astype(brain_float_type), ('dp', 'fsdp'), axis=1...  64 us
    all_gather x1, blocking collectives, on_device(): lax.all_gather(a_down.astype(brain_float_type), ('dp', 'fsdp'), axis=0, t...  63.5 us
    dot_general x11, matrix products, transposed_product(): lax.dot_general(left, right, (((1,), (1,)), ((), ())), preferred_element_...  63.5 us
    all_gather x1, blocking collectives, on_device(): lax.all_gather(a_in.astype(brain_float_type), ('dp', 'fsdp'), axis=0, til...  57.2 us
    dot_general x14, matrix products, product_result(): return jnp.dot(left, right, preferred_element_type=jnp.float32)  47 us
    unnamed x188, local copies, waits for them, and re-layouts  22.4 us
  transfers between devices with their start and end apart: 5, of which 1 were waited for; matrix products, arithmetic and copies ran while one was open for 16% of the time, Pallas kernels for 0%

commit v1 on v0

--- a/solution.py
+++ b/solution.py
@@ -13,6 +13,26 @@
 beta_two = 0.98
 learn_rate = 0.02
 decay_rate = 0.01
+
+
+def point_positions(mat):
+    row_axis = ("dp", "fsdp")
+    all_rows, moved, r2 = (lax.axis_size(row_axis), lax.axis_index(row_axis), mat.shape[1])
+    mat_out, part_now = (mat, 1)
+    while part_now < all_rows:
+        mat_out = jnp.concatenate(
+            [
+                mat_out,
+                lax.ppermute(
+                    mat_out,
+                    row_axis,
+                    [(tick, (tick - part_now) % all_rows) for tick in range(all_rows)],
+                ),
+            ],
+            axis=1,
+        )
+        part_now = 2 * part_now
+    return jnp.roll(mat_out, shift=moved * r2, axis=1)
 
 
 def bucket_plan(full):
@@ -215,7 +235,7 @@
         lax.all_gather(a_in.astype(brain_float_type), ("dp", "fsdp"), axis=0, tiled=True),
         lax.all_gather(a_down.astype(brain_float_type), ("dp", "fsdp"), axis=0, tiled=True),
         lax.all_gather(ln_gains.astype(brain_float_type), ("dp", "fsdp"), axis=1, tiled=True),
-        lax.all_gather(ln_biases.astype(brain_float_type), ("dp", "fsdp"), axis=1, tiled=True),
+        point_positions(ln_biases.astype(brain_float_type)),
     )
     (
         projection_weight_gradient,

time: 659 us -> 614 us (0.932)
  blocking collectives: 251 us -> 184 us
  starting transfers between devices: 0.21 us -> 18 us
    all_gather x1 -> x0, blocking collectives: 64 us -> none  [on_device(): lax.all_gather(ln_biases.astype(brain_float_type), ('dp', 'fsdp'), axis=1...]
    ppermute x0 -> x5, starting transfers between devices: none -> 17.8 us  [point_positions(): lax.ppermute(mat_out, row_axis, [(tick, (tick - part_now) % all_rows) for...]
  transfers between devices with their start and end apart: 5 -> 10, of which waited for: 1 -> 3; matrix products, arithmetic and copies ran while one was open for 16% -> 17% of each run, Pallas kernels for 0% -> 0%
where the time goes in v1:
time: 614 us; the launch traced here: 609 us
  blocking collectives  184 us (30%)
  matrix products  169 us (28%)
  waiting for transfers between devices  124 us (20%)
  local copies, waits for them, and re-layouts  55.2 us (9%)
  other arithmetic  42.4 us (7%)
  starting transfers between devices  18 us (3%)
  between operations  17.3 us (3%)
    psum x1, waiting for transfers between devices, on_device(): b_grad = lax.psum(local_gradient, ('dp', 'fsdp'))  123 us
    all_gather x1, blocking collectives, on_device(): lax.all_gather(ln_gains.astype(brain_float_type), ('dp', 'fsdp'), axis=1,...  64.9 us
    dot_general x11, matrix products, transposed_product(): lax.dot_general(left, right, (((1,), (1,)), ((), ())), preferred_element_...  63.5 us
    all_gather x1, blocking collectives, on_device(): lax.all_gather(a_down.astype(brain_float_type), ('dp', 'fsdp'), axis=0, t...  61.9 us
    all_gather x1, blocking collectives, on_device(): lax.all_gather(a_in.astype(brain_float_type), ('dp', 'fsdp'), axis=0, til...  56.7 us
    dot_general x14, matrix products, product_result(): return jnp.dot(left, right, preferred_element_type=jnp.float32)  48.1 us
    unnamed x188, local copies, waits for them, and re-layouts  22.6 us
    ppermute x5, starting transfers between devices, point_positions(): lax.ppermute(mat_out, row_axis, [(tick, (tick - part_now) % all_rows) for...  17.8 us
  transfers between devices with their start and end apart: 10, of which 3 were waited for; matrix products, arithmetic and copies ran while one was open for 17% of the time, Pallas kernels for 0%

profile of v1, /device:TPU:8, one launch (start us, length us, event | category | flops | bytes accessed | tf_op | source)
XLA Modules:
  0.0 608.8 jit_solution(12405517451787973335)
XLA Ops:
  20.1 56.7 %all_gather.29 = bf16[768,40]{1,0:T(8,128)(2,1)S(1)} all-gather(bf16[24,40]{1,0:T(8,128)(2,1)S(1)} %convert_element_type.393), channel_id=1, replica_groups=mesh['dp'=8,'fsdp'=4] {'dp','fsdp'}, dimensions={0}, use_global_device_ids=true | all-gather | bytes 63360 | tf_op jit(solution)/shard_map/all_gather | solution.py:235
  88.5 64.9 %all-gather = bf16[32,24,2]{1,2,0:T(2,128)(2,1)S(1)} all-gather(bf16[1,24,2]{1,2,0:T(2,128)(2,1)S(1)} %convert_bitcast_fusion.1), channel_id=1, replica_groups=mesh['dp'=8,'fsdp'=4] {'dp','fsdp'}, dimensions={0}, use_global_device_ids=true | all-gather | bytes 3168 | tf_op jit(solution)/shard_map/all_gather | solution.py:237
  156.2 3.9 collective-permute-start.1
  161.5 7.2 %collective-permute-start.2 = (bf16[2,96]{1,0:T(2,128)(2,1)S(1)}, bf16[2,96]{1,0:T(2,128)(2,1)S(1)}, u32[]{:S(2)}, u32[]{:S(2)}) collective-permute-start(bf16[2,96]{1,0:T(2,128)(2,1)S(1)} %pad_maximum_fusion.6), channel_id=1, source_target_pairs={{0,28},{1,29},{2,30},{3,31},{4,0},{5,1},{6,2},{7,3},{8,4},{9,5},{1... | collective-permute-start | bytes 1160 | tf_op jit(solution)/shard_map/ppermute | solution.py:26
  170.0 3.8 collective-permute-start.3
  173.8 61.9 %all-gather.1 = bf16[32,96,8]{1,2,0:T(8,128)(2,1)} all-gather(bf16[1,96,8]{1,2,0:T(8,128)(2,1)S(1)} %convert_bitcast_fusion), channel_id=1, replica_groups=mesh['dp'=8,'fsdp'=4] {'dp','fsdp'}, dimensions={0}, use_global_device_ids=true | all-gather | bytes 50688 | tf_op jit(solution)/shard_map/all_gather | solution.py:236
  242.9 8.9 %fusion.9 = bf16[1024,2304]{1,0:T(8,128)(2,1)} fusion(f32[1024,768]{1,0:T(8,128)} %fusion.119, f32[1024,768]{1,0:T(8,128)} %fusion.122, f32[1024,768]{1,0:T(8,128)} %fusion.125, bf16[1024,768]{1,0:T(8,128)(2,1)S(1)} %copy-done.17, bf16[768,2304]{1,0:T(8,128)(2,1)} %all-gather.7.cloned.1.call-done), kind=kOutput, calls=%fused_computation.20 | convolution fusion | flops 3635675136 | bytes 19267584 | tf_op jit(solution)/shard_map/dot_general | solution.py:58
  251.7 6.7 %copy.151 = bf16[1024,2304]{0,1:T(8,128)(2,1)} copy(bf16[1024,2304]{1,0:T(8,128)(2,1)} %fusion.9) | data formatting | bytes 9437184 | tf_op jit(solution)/shard_map/convert_element_type | solution.py:276
  269.1 5.1 fusion.157
  280.5 4.0 fusion.25
  293.3 7.5 %fusion.162 = f32[1024,3072]{1,0:T(8,128)S(1)} fusion(bf16[1024,768]{0,1:T(8,128)(2,1)} %copy-done.8, bf16[768,3072]{1,0:T(8,128)(2,1)} %all-gather.11.cloned.1.call-done), kind=kOutput, calls=%fused_computation.256 | convolution fusion | flops 4831838208 | bytes 18874368 | tf_op jit(solution)/shard_map/dot_general | solution.py:58
  300.8 6.9 %multiply_convert_fusion.1 = (bf16[1024,3072]{1,0:T(8,128)(2,1)S(1)}, f32[1024,3072]{1,0:T(8,128)}) fusion(f32[1024,3072]{1,0:T(8,128)S(1)} %fusion.162, bf16[1024,8]{0,1:T(8,128)(2,1)S(1)} %convolution_convert_fusion.6, bf16[8,6912]{1,0:T(8,128)(2,1)S(1)} %convert_element_type.395), kind=kOutput, calls=%fused_computation.10 | convolution fusion | flops 72351744 | bytes 31522816 | tf_op jit(solution)/shard_map/dot_general | solution.py:58
  312.2 8.8 %fusion.163 = f32[1024,768]{0,1:T(8,128)S(1)} fusion(bf16[1024,3072]{1,0:T(8,128)(2,1)} %copy-done.6, bf16[3072,768]{1,0:T(8,128)(2,1)} %all-gather.13.cloned.1.call-done), kind=kOutput, calls=%fused_computation.257 | convolution fusion | flops 4831838208 | bytes 14155776 | tf_op jit(solution)/shard_map/dot_general | solution.py:58
  328.2 8.1 %fusion.164 = f32[1024,3072]{1,0:T(8,128)} fusion(bf16[1024,768]{0,1:T(8,128)(2,1)S(1)} %get-tuple-element.118, bf16[3072,768]{1,0:T(8,128)(2,1)S(1)} %bitcast.272), kind=kOutput, calls=%fused_computation.258 | convolution fusion | flops 4831838208 | bytes 18874368 | tf_op jit(solution)/shard_map/dot_general | solution.py:62
  336.2 13.7 %fusion.5 = bf16[1024,3072]{1,0:T(8,128)(2,1)} fusion(f32[1024,3072]{1,0:T(8,128)} %get-tuple-element.136, f32[1024,3072]{1,0:T(8,128)} %fusion.164, bf16[3072,8]{0,1:T(8,128)(2,1)S(1)} %copy-done.47, bf16[1024,768]{0,1:T(8,128)(2,1)} %copy-done.18, bf16[8,6912]{1,0:T(8,128)(2,1)S(1)} %convert_element_type.395), kind=kOutput, calls=%fused_computation.6 | convolution fusion | flops 97533952 | bytes 33091584 | tf_op jit(solution)/shard_map/dot_general | solution.py:62
  349.9 10.0 %fusion.165 = f32[1024,768]{0,1:T(8,128)} fusion(bf16[1024,3072]{1,0:T(8,128)(2,1)} %fusion.5, bf16[768,3072]{1,0:T(8,128)(2,1)} %all-gather.11.cloned.1.call-done), kind=kOutput, calls=%fused_computation.259 | convolution fusion | flops 4831838208 | bytes 14155776 | tf_op jit(solution)/shard_map/dot_general | solution.py:62
  359.9 10.3 %fusion.149 = (f32[1024]{0:T(1024)S(1)}, f32[1024]{0:T(1024)S(1)}, f32[1024,768]{0,1:T(8,128)}) fusion(f32[1024]{0:T(1024)S(1)} %copy-done.53, f32[1024,768]{0,1:T(8,128)S(1)} %get-tuple-element.134, f32[1024]{0:T(1024)S(1)} %broadcast_multiply_fusion.6, f32[768]{0:T(1024)S(1)} %copy-done.62, bf16[768,40]{1,0:T(8,128)(2,1)S(1)} %all_gather.29, ...), kind=kOutput, calls=%fused_computation.246 | convolution fusion | flops 76298240 | bytes 20738048 | tf_op jit(solution)/shard_map/dot_general | solution.py:62
  377.2 4.4 add_convert_fusion.1
  410.1 3.2 fusion.38
  413.3 7.2 %multiply_reduce_fusion = (f32[12,512]{1,0:T(8,128)S(1)}, f32[12,512,512]{1,2,0:T(8,128)}) fusion(f32[12,512,512]{1,2,0:T(8,128)S(1)} %bitcast.233, f32[12,512]{1,0:T(8,128)S(1)} %copy-done.39, bf16[512,12,64]{0,2,1:T(8,128)(2,1)S(1)} %bitcast.260, bf16[1,1024,3,12,64]{1,4,3,2,0:T(8,128)(2,1)} %bitcast.247), kind=kOutput, calls=%fused_computation.8 | convolution fusion | flops 412084224 | bytes 26787840 | tf_op jit(solution)/shard_map/while/body/eval_jaxpr/gqhe,gkhe->ghqk/dot_general | solution.py:122
  420.5 6.8 %multiply_convert_fusion = bf16[12,512,512]{1,2,0:T(8,128)(2,1)S(1)} fusion(f32[12,512,512]{1,2,0:T(8,128)} %get-tuple-element.147, f32[12,512,512]{1,2,0:T(8,128)S(1)} %bitcast.233, f32[12,512]{1,0:T(8,128)S(1)} %get-tuple-element.146, f32[12,512]{1,0:T(8,128)S(1)} %copy-done.39), kind=kLoop, calls=%fused_computation.7 | loop fusion | flops 12582912 | bytes 31506432 | tf_op jit(solution)/shard_map/while/body/eval_jaxpr/convert_element_type | solution.py:126
  427.3 4.0 fusion.43
  458.1 6.9 %fusion.167 = f32[1024,768]{0,1:T(8,128)S(1)} fusion(bf16[768,2304]{1,0:T(8,128)(2,1)} %all-gather.7.cloned.1.call-done, bf16[1024,2304]{0,1:T(8,128)(2,1)} %bitcast.258), kind=kOutput, calls=%fused_computation.261 | convolution fusion | flops 3623878656 | bytes 11403264 | tf_op jit(solution)/shard_map/dot_general | solution.py:62
  471.6 123.2 %all-reduce.2.cloned.1.call-done = f32[8,6912]{1,0:T(8,128)} async-done(((f32[8,6912]{1,0:T(8,128)}), f32[8,6912]{1,0:T(8,128)}) %all-reduce.2.cloned.1.call-update) | async-done | bytes 221200 | tf_op jit(solution)/shard_map/psum | solution.py:399
  (336 shorter events, 147.5 us)
Async XLA Ops:
  7.2 235.7 %all-gather.7.cloned.1.call-start = ((), (), s32[]{:S(2)}) async-start(), calls=%async_computation | async-start | bytes 3649536 | tf_op jit(solution)/shard_map/all_gather | solution.py:229
  8.8 276.1 %all-gather.9.cloned.1.call-start = ((), (), s32[]{:S(2)}) async-start(), calls=%async_computation.1 | async-start | bytes 1216512 | tf_op jit(solution)/shard_map/all_gather | solution.py:232
  10.4 282.9 %all-gather.11.cloned.1.call-start = ((), (), s32[]{:S(2)}) async-start(), calls=%async_computation.2 | async-start | bytes 4866048 | tf_op jit(solution)/shard_map/all_gather | solution.py:233
  12.1 300.0 %all-gather.13.cloned.1.call-start = ((), (), s32[]{:S(2)}) async-start(), calls=%async_computation.3 | async-start | bytes 4866048 | tf_op jit(solution)/shard_map/all_gather | solution.py:234
  12.9 143.2 %collective-permute-start = (bf16[2,24]{1,0:T(2,128)(2,1)S(1)}, bf16[2,24]{1,0:T(2,128)(2,1)S(1)}, u32[]{:S(2)}, u32[]{:S(2)}) collective-permute-start(bf16[2,24]{1,0:T(2,128)(2,1)S(1)} %convert_element_type.420), channel_id=1, source_target_pairs={{0,31},{1,0},{2,1},{3,2},{4,3},{5,4},{6,5},{7,6},{8,7},{9,8},{10,9... | collective-permute-start | bytes 296 | tf_op jit(solution)/shard_map/ppermute | solution.py:26
  16.3 578.6 %all-reduce.2.cloned.1.call-start = ((), (), s32[]{:S(2)}) async-start(), calls=%async_computation.4 | async-start | bytes 442368 | tf_op jit(solution)/shard_map/psum | solution.py:399
  20.1 357.1 %copy-start.38 = (bf16[8,6912]{1,0:T(8,128)(2,1)}, bf16[8,6912]{1,0:T(8,128)(2,1)S(1)}, u32[]{:S(2)}) copy-start(bf16[8,6912]{1,0:T(8,128)(2,1)S(1)} %convert_element_type.395) | copy-start | bytes 331780
  81.1 155.9 %copy-start.17 = (bf16[1024,768]{1,0:T(8,128)(2,1)S(1)}, bf16[1024,768]{1,0:T(8,128)(2,1)}, u32[]{:S(2)}) copy-start(bf16[1024,768]{1,0:T(8,128)(2,1)} %param.14) | copy-start | bytes 4718596
  83.4 157.0 %copy-start.26 = (bf16[1024,768]{1,0:T(8,128)(2,1)S(1)}, bf16[1024,768]{1,0:T(8,128)(2,1)}, u32[]{:S(2)}) copy-start(bf16[1024,768]{1,0:T(8,128)(2,1)} %param.15) | copy-start | bytes 4718596
  154.3 136.9 %copy-start.61 = (f32[768]{0:T(1024)}, f32[768]{0:T(1024)S(1)}, u32[]{:S(2)}) copy-start(f32[768]{0:T(1024)S(1)} %get-tuple-element.109) | copy-start | bytes 9220
  156.2 5.2 collective-permute-start.1
  161.5 8.5 %collective-permute-start.2 = (bf16[2,96]{1,0:T(2,128)(2,1)S(1)}, bf16[2,96]{1,0:T(2,128)(2,1)S(1)}, u32[]{:S(2)}, u32[]{:S(2)}) collective-permute-start(bf16[2,96]{1,0:T(2,128)(2,1)S(1)} %pad_maximum_fusion.6), channel_id=1, source_target_pairs={{0,28},{1,29},{2,30},{3,31},{4,0},{5,1},{6,2},{7,3},{8,4},{9,5},{1... | collective-permute-start | bytes 1160 | tf_op jit(solution)/shard_map/ppermute | solution.py:26
  170.0 65.8 %collective-permute-start.3 = (bf16[2,192]{1,0:T(2,128)(2,1)S(1)}, bf16[2,192]{1,0:T(2,128)(2,1)S(1)}, u32[]{:S(2)}, u32[]{:S(2)}) collective-permute-start(bf16[2,192]{1,0:T(2,128)(2,1)S(1)} %pad_maximum_fusion.4), channel_id=1, source_target_pairs={{0,24},{1,25},{2,26},{3,27},{4,28},{5,29},{6,30},{7,31},{8,0},{9,1... | collective-permute-start | bytes 2312 | tf_op jit(solution)/shard_map/ppermute | solution.py:26
  235.8 6.2 %collective-permute-start.4 = (bf16[2,384]{1,0:T(2,128)(2,1)S(1)}, bf16[2,384]{1,0:T(2,128)(2,1)S(1)}, u32[]{:S(2)}, u32[]{:S(2)}) collective-permute-start(bf16[2,384]{1,0:T(2,128)(2,1)S(1)} %concatenate.73), channel_id=1, source_target_pairs={{0,16},{1,17},{2,18},{3,19},{4,20},{5,21},{6,22},{7,23},{8,24},{9,... | collective-permute-start | bytes 4616 | tf_op jit(solution)/shard_map/ppermute | solution.py:26
  288.7 81.4 %copy-start.45 = (f32[1024]{0:T(1024)}, f32[1024]{0:T(1024)S(1)}, u32[]{:S(2)}) copy-start(f32[1024]{0:T(1024)S(1)} %broadcast_multiply_fusion.6) | copy-start | bytes 12292
  300.8 9.6 %copy-start.47 = (bf16[3072,8]{0,1:T(8,128)(2,1)S(1)}, bf16[3072,8]{0,1:T(8,128)(2,1)}, u32[]{:S(2)}) copy-start(bf16[3072,8]{0,1:T(8,128)(2,1)} %reshape.754) | copy-start | bytes 147460
  312.1 8.9 %copy-start.50 = (bf16[1024,8]{0,1:T(8,128)(2,1)}, bf16[1024,8]{0,1:T(8,128)(2,1)S(1)}, u32[]{:S(2)}) copy-start(bf16[1024,8]{0,1:T(8,128)(2,1)S(1)} %convolution_convert_fusion.5) | copy-start | bytes 49156
  312.1 8.9 %copy-start.53 = (f32[1024]{0:T(1024)S(1)}, f32[1024]{0:T(1024)}, u32[]{:S(2)}) copy-start(f32[1024]{0:T(1024)} %copy-done.52) | copy-start | bytes 12292
  312.1 8.9 %copy-start.62 = (f32[768]{0:T(1024)S(1)}, f32[768]{0:T(1024)}, u32[]{:S(2)}) copy-start(f32[768]{0:T(1024)} %copy-done.61) | copy-start | bytes 9220
  312.1 8.9 %copy-start.69 = (f32[768]{0:T(1024)S(1)}, f32[768]{0:T(1024)}, u32[]{:S(2)}) copy-start(f32[768]{0:T(1024)} %get-tuple-element.111) | copy-start | bytes 9220
  434.5 10.7 %copy-start.33 = (bf16[128,12,64]{0,2,1:T(8,128)(2,1)S(1)}, bf16[128,12,64]{0,2,1:T(8,128)(2,1)}, u32[]{:S(2)}) copy-start(bf16[128,12,64]{0,2,1:T(8,128)(2,1)} %fusion.66) | copy-start | bytes 589828
  467.3 129.8 %copy-start.32 = (f32[8,6912]{1,0:T(8,128)S(1)}, f32[8,6912]{1,0:T(8,128)}, u32[]{:S(2)}) copy-start(f32[8,6912]{1,0:T(8,128)} %param.25) | copy-start | bytes 663556
  467.3 129.9 %copy-start.43 = (f32[8,6912]{1,0:T(8,128)S(1)}, f32[8,6912]{1,0:T(8,128)}, u32[]{:S(2)}) copy-start(f32[8,6912]{1,0:T(8,128)} %param.27) | copy-start | bytes 663556
  467.3 129.9 %copy-start.44 = (f32[8,6912]{1,0:T(8,128)S(1)}, f32[8,6912]{1,0:T(8,128)}, u32[]{:S(2)}) copy-start(f32[8,6912]{1,0:T(8,128)} %param.26) | copy-start | bytes 663556
  (77 other events, 290.5 us)
Sparse Core Ops, SparseCore 0:
  11.4 60.8 all-gather.6
  75.2 52.6 all-gather.8
  131.4 63.4 all-gather.10
  198.2 61.8 all-gather.12
  458.2 136.6 all-reduce.1
